TPU v7x, 32 devices: a whole 2x2x4 slice. The times are simulated.
32 devices in a mesh: member: 2 (over y), slab: 4 (over z), chan: 2 (over x), mode: 2 (over core).
Axes of the slice: x: 2, y: 2, z: 4, core: 2. Of those that a mesh axis runs over, the one named last changes fastest.
Arguments:
- source_field: float32 [128, 1024, 1024], P(('member', 'chan'), 'slab', 'mode'), parts along dimension 0, may hold values from -6 to 6
- cotangent: float32 [128, 1024, 1024], P(('member', 'chan'), 'slab', 'mode'), parts along dimension 0, may hold values from -6 to 6
- spectral_weight: float32 [128, 64, 32, 2, 64], P(('member', 'chan'), None, 'mode', None, 'slab'), parts along dimension 0, may hold values from -12 to 12
- skip_gain: float32 [128], P(('member', 'chan')), parts along dimension 0, may hold values from 0.5 to 2
- channel_bias: float32 [128], P(('member', 'chan')), parts along dimension 0, may hold values from -0.5 to 0.5
- mode_limit: int32 [128, 2], P('member'), parts along dimension 0, may hold values from 16 to 32
- width_limit: int32 [128], P('member'), parts along dimension 0, may hold values from 32 to 64
Outputs:
- output: float32 [128, 1024, 1024], P(('member', 'chan'), 'slab', 'mode'), parts along dimension 0
- field_grad: float32 [128, 1024, 1024], P(('member', 'chan'), 'slab', 'mode'), parts along dimension 0
- spectral_grad: float32 [128, 64, 32, 2, 64], P(('member', 'chan'), None, 'mode', None, 'slab'), parts along dimension 0
- gate_grad: float32 [128], P(('member', 'chan')), parts along dimension 0
- bias_grad: float32 [128], P(('member', 'chan')), parts along dimension 0
There are 2 independent parts, one for each index of `member`. A program takes and returns all parts, laid end to end along the dimension named above; each array names one. Nothing has to cross between parts.
Inputs may be any that keep to these rules, and one draw needn't show every extreme that they name: `mode_limit`: never more than 32. `width_limit`: never more than 64.
All inputs are finite; a program needn't handle non-finite values.
Results may differ from a plain program's by a relative error of at most 0.00018.
Values sent between devices are 32-bit elements; how exact they have to be, the bound alone decides.
A program may use at most 192 MiB of HBM per device.

v0:
```python
import math

import jax
import jax.numpy as jnp
from jax import lax
from jax.sharding import PartitionSpec as P

precise = lax.Precision.HIGHEST


def column_table(extent, freq_count, first_cell, cell_count):
    cell_index = first_cell + jnp.arange(cell_count, dtype=jnp.int32)
    wave_index = jnp.arange(freq_count, dtype=jnp.int32)
    products = (cell_index[:, None] * wave_index[None, :] % extent).astype(jnp.float32)
    angles = products * (2.0 * math.pi / extent)
    return jnp.stack([jnp.cos(angles), -jnp.sin(angles)], axis=-1).reshape(
        cell_count, 2 * freq_count
    )


def row_tables(extent, freq_count, first_cell, cell_count):
    cell_index = first_cell + jnp.arange(cell_count, dtype=jnp.int32)
    column = jnp.arange(2 * freq_count, dtype=jnp.int32)
    wave_index = column + jnp.where(column >= freq_count, extent - 2 * freq_count, 0)
    products = (cell_index[:, None] * wave_index[None, :] % extent).astype(jnp.float32)
    angles = products * (2.0 * math.pi / extent)
    return (jnp.cos(angles), jnp.sin(angles))


def row_forward(lined, row_cos, row_sin):
    line_real = lined[:, 0]
    line_imag = lined[:, 1]
    out_real = jnp.dot(line_real, row_cos, precision=precise) + jnp.dot(
        line_imag, row_sin, precision=precise
    )
    out_imag = jnp.dot(line_imag, row_cos, precision=precise) - jnp.dot(
        line_real, row_sin, precision=precise
    )
    return jnp.stack([out_real, out_imag], axis=1)


def row_inverse(modes_in, row_cos, row_sin):
    mode_real = modes_in[:, 0]
    mode_imag = modes_in[:, 1]
    back_real = jnp.dot(mode_real, row_cos.T, precision=precise) - jnp.dot(
        mode_imag, row_sin.T, precision=precise
    )
    back_imag = jnp.dot(mode_real, row_sin.T, precision=precise) + jnp.dot(
        mode_imag, row_cos.T, precision=precise
    )
    return jnp.stack([back_real, back_imag], axis=1)


def contract(spectra, weight):
    spec_real = spectra[:, :, 0]
    spec_imag = spectra[:, :, 1]
    weight_real = weight[:, :, :, 0]
    weight_imag = weight[:, :, :, 1]
    out_real = jnp.einsum("iyx,ioyx->oyx", spec_real, weight_real, precision=precise) - jnp.einsum(
        "iyx,ioyx->oyx", spec_imag, weight_imag, precision=precise
    )
    out_imag = jnp.einsum("iyx,ioyx->oyx", spec_real, weight_imag, precision=precise) + jnp.einsum(
        "iyx,ioyx->oyx", spec_imag, weight_real, precision=precise
    )
    return jnp.stack([out_real, out_imag], axis=2)


def contract_back(grads, weight):
    grad_real = grads[:, :, 0]
    grad_imag = grads[:, :, 1]
    weight_real = weight[:, :, :, 0]
    weight_imag = weight[:, :, :, 1]
    back_real = jnp.einsum("oyx,ioyx->iyx", grad_real, weight_real, precision=precise) + jnp.einsum(
        "oyx,ioyx->iyx", grad_imag, weight_imag, precision=precise
    )
    back_imag = jnp.einsum("oyx,ioyx->iyx", grad_imag, weight_real, precision=precise) - jnp.einsum(
        "oyx,ioyx->iyx", grad_real, weight_imag, precision=precise
    )
    return jnp.stack([back_real, back_imag], axis=2)


def outer_grad(spectra, grads):
    spec_real = spectra[:, :, 0]
    spec_imag = spectra[:, :, 1]
    grad_real = grads[:, :, 0]
    grad_imag = grads[:, :, 1]
    real_side = jnp.einsum("iyx,oyx->ioyx", spec_real, grad_real) + jnp.einsum(
        "iyx,oyx->ioyx", spec_imag, grad_imag
    )
    imag_side = jnp.einsum("iyx,oyx->ioyx", spec_real, grad_imag) - jnp.einsum(
        "iyx,oyx->ioyx", spec_imag, grad_real
    )
    return jnp.stack([real_side, imag_side], axis=3)


def mode_weights(limit_rows, col_freq, row_freq, kx_count, cells_total):
    keep_cols = col_freq[None, :] < limit_rows[:, 0:1]
    keep_rows = (row_freq[None, :] < limit_rows[:, 1:2]) | (
        (kx_count - row_freq)[None, :] < limit_rows[:, 1:2]
    )
    scales = jnp.where(col_freq == 0, 1.0, 2.0).astype(jnp.float32) / cells_total
    joined = keep_cols[:, :, None] & keep_rows[:, None, :]
    return (joined.astype(jnp.float32) * scales[None, :, None])[:, :, None, :]


def read_mask(in_index, width_limit):
    return (in_index[:, None] < width_limit[None, :]).astype(jnp.float32)[:, :, None, None, None]


def local(
    source_field, cotangent, spectral_weight, skip_gain, channel_bias, mode_limit, width_limit
):
    channels, row_count, col_count = source_field.shape
    slab_count = lax.axis_size("slab")
    mode_count = lax.axis_size("mode")
    slab_index = lax.axis_index("slab")
    mode_index = lax.axis_index("mode")
    chan_index = lax.axis_index("chan")
    local_freq = spectral_weight.shape[2]
    local_kx = spectral_weight.shape[4]
    freq_count = local_freq * mode_count
    kx_count = local_kx * slab_count
    all_rows = row_count * slab_count
    all_cols = col_count * mode_count
    column_tab = column_table(all_cols, freq_count, mode_index * col_count, col_count)
    row_cos, row_sin = row_tables(all_rows, freq_count, slab_index * row_count, row_count)

    def spectrum(values):
        partial_cols = jnp.einsum("chw,wk->ckh", values, column_tab, precision=precise)
        summed_cols = lax.psum_scatter(partial_cols, "mode", scatter_dimension=1, tiled=True)
        paired = summed_cols.reshape(values.shape[0] * local_freq, 2, row_count)
        spectra = lax.psum_scatter(
            row_forward(paired, row_cos, row_sin), "slab", scatter_dimension=2, tiled=True
        )
        return spectra.reshape(values.shape[0], local_freq, 2, local_kx)

    def synthesis(modes_in):
        whole_modes = lax.all_gather(modes_in, "slab", axis=3, tiled=True)
        rebuilt = row_inverse(
            whole_modes.reshape(channels * local_freq, 2, kx_count), row_cos, row_sin
        )
        rebuilt = rebuilt.reshape(channels, 2 * local_freq, row_count)
        gathered = lax.all_gather(rebuilt, "mode", axis=1, tiled=True)
        return jnp.einsum("ckh,wk->chw", gathered, column_tab, precision=precise)

    in_index = chan_index * channels + jnp.arange(channels, dtype=jnp.int32)
    col_freq = mode_index * local_freq + jnp.arange(local_freq, dtype=jnp.int32)
    row_freq = slab_index * local_kx + jnp.arange(local_kx, dtype=jnp.int32)
    limit_rows = lax.dynamic_slice_in_dim(mode_limit, chan_index * channels, channels, 0)
    weights = mode_weights(limit_rows, col_freq, row_freq, kx_count, all_rows * all_cols)
    reads = read_mask(in_index, width_limit)
    masked_weight = spectral_weight * reads
    spectra = spectrum(source_field)
    out_modes = (
        lax.psum_scatter(contract(spectra, masked_weight), "chan", scatter_dimension=0, tiled=True)
        * weights
    )
    branch = synthesis(out_modes)
    skip_scale = skip_gain[:, None, None]
    summed = branch + skip_scale * source_field + channel_bias[:, None, None]
    output, gelu_back = jax.vjp(jax.nn.gelu, summed)
    grad_sum = gelu_back(cotangent)[0]
    grad_modes = spectrum(grad_sum) * weights
    all_grads = lax.all_gather(grad_modes, "chan", axis=0, tiled=True)
    spectral_grad = outer_grad(spectra, all_grads) * reads
    field_grad = synthesis(contract_back(all_grads, masked_weight)) + skip_scale * grad_sum
    gate_grad, bias_grad = lax.psum(
        (jnp.sum(grad_sum * source_field, axis=(1, 2)), jnp.sum(grad_sum, axis=(1, 2))),
        ("slab", "mode"),
    )
    return (output, field_grad, spectral_grad, gate_grad, bias_grad)


def solution(mesh):
    in_specs = (
        P(("member", "chan"), "slab", "mode"),
        P(("member", "chan"), "slab", "mode"),
        P(("member", "chan"), None, "mode", None, "slab"),
        P(("member", "chan")),
        P(("member", "chan")),
        P("member", None),
        P("member"),
    )
    out_specs = (
        P(("member", "chan"), "slab", "mode"),
        P(("member", "chan"), "slab", "mode"),
        P(("member", "chan"), None, "mode", None, "slab"),
        P(("member", "chan")),
        P(("member", "chan")),
    )
    return jax.shard_map(local, mesh=mesh, in_specs=in_specs, out_specs=out_specs, check_vma=False)
```

profile of v0, /device:TPU:0, one launch (start us, length us, event | category | flops | bytes accessed | tf_op | source)
XLA Modules:
  0.0 418.1 jit_solution(5773580187036393755)
XLA Ops:
  7.8 20.7 %convolution_bitcast_fusion.1 = f32[32,64,256]{2,1,0:T(8,128)} fusion(f32[512,64,1]{0,1,2:T(8,128)S(1)} %reshape.294, f32[32,256,512]{2,1,0:T(8,128)} %param.7), kind=kOutput, calls=%fused_computation.35 | convolution fusion | flops 3221225472 | bytes 19005440 | tf_op jit(solution)/shard_map/chw,wk->ckh/dot_general | solution.py:129
  29.8 8.5 %broadcast_multiply_fusion = f32[32,64,16,2,16]{1,4,3,2,0:T(8,128)} fusion(f32[32,64,16,2,16]{1,4,3,2,0:T(8,128)} %param.9, f32[32,64]{1,0:T(8,128)S(1)} %compare_convert_fusion), kind=kLoop, calls=%fused_computation.17 | loop fusion | flops 1048576 | bytes 8396800 | tf_op jit(solution)/shard_map/mul | solution.py:152
  38.3 2.7 reduce-scatter.6.cloned.1.call-done
  41.0 1.8 reshape.286
  43.7 1.2 fusion.40
  44.9 1.2 fusion.36
  46.1 1.2 fusion.29
  47.3 1.2 fusion.28
  49.5 7.8 %slice_bitcast_fusion.1 = (f32[32,64,16,16]{1,3,2,0:T(8,128)}, f32[32,64,16,16]{1,3,2,0:T(8,128)}) fusion(f32[32,64,16,2,16]{1,4,3,2,0:T(8,128)} %broadcast_multiply_fusion), kind=kLoop, calls=%fused_computation.14 | loop fusion | bytes 8388608 | tf_op jit(solution)/shard_map/squeeze | solution.py:57
  57.3 13.4 %reduce-scatter.8.cloned.1.call-done = f32[512,2,16]{0,2,1:T(8,128)} async-done(((f32[512,2,64]{0,2,1:T(8,128)}), f32[512,2,16]{0,2,1:T(8,128)}) %reduce-scatter.8.cloned.1.call-update) | async-done | bytes 65552 | tf_op jit(solution)/shard_map/reduce_scatter | solution.py:132
  72.1 8.3 %fusion.18 = f32[16,16,1,64]{3,2,1,0:T(1,128)S(1)} fusion(f32[32,16,16,1]{0,3,2,1:T(1,128)S(1)} %copy.60, f32[32,64,16,16]{1,3,2,0:T(8,128)} %get-tuple-element.11), kind=kOutput, calls=%fused_computation.30 | convolution fusion | flops 6291456 | bytes 2195456 | tf_op jit(solution)/shard_map/iyx,ioyx->oyx/dot_general | solution.py:62
  80.5 8.6 %fusion.12 = f32[16,16,1,64]{3,2,1,0:T(1,128)S(1)} fusion(f32[32,16,16,1]{0,3,2,1:T(1,128)S(1)} %copy.60, f32[32,64,16,16]{1,3,2,0:T(8,128)} %get-tuple-element.12), kind=kOutput, calls=%fused_computation.24 | convolution fusion | flops 6291456 | bytes 2195456 | tf_op jit(solution)/shard_map/iyx,ioyx->oyx/dot_general | solution.py:59
  89.1 6.0 %fusion.20 = f32[16,16,1,64]{3,2,1,0:T(1,128)S(1)} fusion(f32[32,16,16,1]{0,3,2,1:T(1,128)S(1)} %copy.57, f32[32,64,16,16]{1,3,2,0:T(8,128)S(1)} %copy-done.3), kind=kOutput, calls=%fused_computation.32 | convolution fusion | flops 6291456 | bytes 2195456 | tf_op jit(solution)/shard_map/iyx,ioyx->oyx/dot_general | solution.py:59
  95.2 6.2 %fusion.10 = f32[16,16,1,64]{3,2,1,0:T(1,128)S(1)} fusion(f32[32,16,16,1]{0,3,2,1:T(1,128)S(1)} %copy.57, f32[32,64,16,16]{1,3,2,0:T(8,128)S(1)} %copy-done.2), kind=kOutput, calls=%fused_computation.22 | convolution fusion | flops 6291456 | bytes 2195456 | tf_op jit(solution)/shard_map/iyx,ioyx->oyx/dot_general | solution.py:62
  101.5 1.3 copy.46
  103.0 18.5 %reduce-scatter.10.cloned.1.call-done = f32[32,16,2,16]{1,0,3,2:T(8,128)} async-done(((f32[64,16,2,16]{1,0,3,2:T(8,128)}), f32[32,16,2,16]{1,0,3,2:T(8,128)}) %reduce-scatter.10.cloned.1.call-update) | async-done | bytes 65552 | tf_op jit(solution)/shard_map/reduce_scatter | solution.py:155
  122.7 38.4 %all_gather.15 = f32[32,16,2,64]{1,0,3,2:T(8,128)S(1)} all-gather(f32[32,16,2,16]{1,0,3,2:T(8,128)S(1)} %broadcast_multiply_fusion.2), channel_id=1, replica_groups=mesh['member'=2,'slab'=4,'chan'=2,'mode'=2] {'slab'}, dimensions={3}, use_global_device_ids=true | all-gather | bytes 327680 | tf_op jit(solution)/shard_map/all_gather | solution.py:138
  161.2 1.3 copy.47
  162.5 1.1 fusion.50
  163.6 1.1 fusion.51
  164.8 1.1 fusion.24
  165.9 1.1 fusion.25
  167.9 1.7 reshape.289
  169.7 11.1 %all-gather.3.cloned.1.call-done = f32[32,64,256]{2,1,0:T(8,128)} async-done(((f32[32,32,256]{2,1,0:T(8,128)}), f32[32,64,256]{2,1,0:T(8,128)}) %all-gather.3.cloned.1.call-update) | async-done | bytes 2097168 | tf_op jit(solution)/shard_map/all_gather | solution.py:143
  180.9 36.1 %fusion.150 = (f32[32]{0:T(128)}, f32[32]{0:T(128)}, f32[32,256,512]{2,1,0:T(8,128)S(1)}, f32[32,256,512]{2,1,0:T(8,128)}) fusion(f32[32,256,512]{2,1,0:T(8,128)} %param.7, f32[32,256,512]{2,1,0:T(8,128)} %param.8, f32[32]{0:T(128)S(1)} %copy-done.9, f32[32]{0:T(128)S(1)} %copy-done.7, f32[32,64,256]{2,1,0:T(8,128)} %all-gather.3.cloned.1.call-done, ...), kind=kOutput, calls=%fused_computation.205 | convolution fusion | flops 3330277376 | bytes 69337600 | tf_op jit(solution)/shard_map/ckh,wk->chw/dot_general | solution.py:144
  216.9 6.2 %copy-done.4 = f32[32,256,512]{2,1,0:T(8,128)} copy-done((f32[32,256,512]{2,1,0:T(8,128)}, f32[32,256,512]{2,1,0:T(8,128)S(1)}, u32[]{:S(2)}) %copy-start.4) | copy-done | bytes 16777240
  223.1 17.8 %convolution_bitcast_fusion = f32[32,64,256]{2,1,0:T(8,128)} fusion(f32[512,64,1]{0,1,2:T(8,128)S(1)} %reshape.294, f32[32,256,512]{2,1,0:T(8,128)S(1)} %get-tuple-element.9), kind=kOutput, calls=%fused_computation.34 | convolution fusion | flops 3221225472 | bytes 19005440 | tf_op jit(solution)/shard_map/chw,wk->ckh/dot_general | solution.py:129
  241.0 10.9 %reduce-scatter.12.cloned.1.call-done = f32[32,32,256]{2,1,0:T(8,128)} async-done(((f32[32,64,256]{2,1,0:T(8,128)}), f32[32,32,256]{2,1,0:T(8,128)}) %reduce-scatter.12.cloned.1.call-update) | async-done | bytes 1048592 | tf_op jit(solution)/shard_map/reduce_scatter | solution.py:130
  251.9 1.8 reshape.290
  254.5 1.2 fusion.34
  255.7 1.2 fusion.30
  256.9 1.2 fusion.27
  258.1 1.2 fusion.26
  260.1 21.4 %reduce-scatter.14.cloned.1.call-done = f32[512,2,16]{0,2,1:T(8,128)} async-done(((f32[512,2,64]{0,2,1:T(8,128)}), f32[512,2,16]{0,2,1:T(8,128)}) %reduce-scatter.14.cloned.1.call-update) | async-done | bytes 65552 | tf_op jit(solution)/shard_map/reduce_scatter | solution.py:132
  282.6 11.9 %all_gather.17 = f32[64,16,2,16]{1,0,3,2:T(8,128)S(1)} all-gather(f32[32,16,2,16]{1,0,3,2:T(8,128)S(1)} %broadcast_multiply_fusion.1), channel_id=1, replica_groups=mesh['member'=2,'slab'=4,'chan'=2,'mode'=2] {'chan'}, dimensions={0}, use_global_device_ids=true | all-gather | bytes 196608 | tf_op jit(solution)/shard_map/all_gather | solution.py:164
  295.0 11.1 %fusion.16 = f32[16,16,1,32]{3,2,1,0:T(1,128)S(1)} fusion(f32[64,16,16,1]{0,3,2,1:T(1,128)S(1)} %copy.64, f32[32,64,16,16]{1,3,2,0:T(8,128)} %get-tuple-element.11), kind=kOutput, calls=%fused_computation.28 | convolution fusion | flops 6291456 | bytes 2195456 | tf_op jit(solution)/shard_map/oyx,ioyx->iyx/dot_general | solution.py:73
  306.0 10.9 %fusion.6 = f32[16,16,1,32]{3,2,1,0:T(1,128)S(1)} fusion(f32[64,16,16,1]{0,3,2,1:T(1,128)S(1)} %copy.64, f32[32,64,16,16]{1,3,2,0:T(8,128)} %get-tuple-element.12), kind=kOutput, calls=%fused_computation.18 | convolution fusion | flops 6291456 | bytes 2195456 | tf_op jit(solution)/shard_map/oyx,ioyx->iyx/dot_general | solution.py:76
  317.1 11.1 %fusion.14 = f32[16,16,1,32]{3,2,1,0:T(1,128)S(1)} fusion(f32[64,16,16,1]{0,3,2,1:T(1,128)S(1)} %copy.66, f32[32,64,16,16]{1,3,2,0:T(8,128)} %get-tuple-element.11), kind=kOutput, calls=%fused_computation.26 | convolution fusion | flops 6291456 | bytes 2195456 | tf_op jit(solution)/shard_map/oyx,ioyx->iyx/dot_general | solution.py:76
  328.2 10.9 %fusion.8 = f32[16,16,1,32]{3,2,1,0:T(1,128)S(1)} fusion(f32[64,16,16,1]{0,3,2,1:T(1,128)S(1)} %copy.66, f32[32,64,16,16]{1,3,2,0:T(8,128)} %get-tuple-element.12), kind=kOutput, calls=%fused_computation.20 | convolution fusion | flops 6291456 | bytes 2195456 | tf_op jit(solution)/shard_map/oyx,ioyx->iyx/dot_general | solution.py:73
  339.3 19.9 %all_gather.18 = f32[32,16,2,64]{0,1,2,3:T(8,128)S(1)} all-gather(f32[32,16,2,16]{0,1,2,3:T(8,128)S(1)} %pad_maximum_fusion.5), channel_id=1, replica_groups=mesh['member'=2,'slab'=4,'chan'=2,'mode'=2] {'slab'}, dimensions={3}, use_global_device_ids=true | all-gather | bytes 327680 | tf_op jit(solution)/shard_map/all_gather | solution.py:138
  361.2 1.1 fusion.53
  362.4 1.1 fusion.22
  363.5 1.1 fusion.23
  365.5 1.7 reshape.293
  367.7 14.5 %all-reduce = (f32[32]{0:T(128)}, f32[32]{0:T(128)}) all-reduce(f32[32]{0:T(128)} %get-tuple-element.6, f32[32]{0:T(128)S(1)} %copy-done.10), channel_id=1, replica_groups=mesh['member'=2,'slab'=4,'chan'=2,'mode'=2] {'slab','mode'}, use_global_device_ids=true, to_apply=%region_6.7 | all-reduce | flops 64 | bytes 512 | tf_op jit(solution)/shard_map/psum | solution.py:167
  382.6 2.3 add_bitcast_fusion
  385.0 4.5 %maximum_multiply_fusion = f32[32,64,16,2,16]{1,4,3,2,0:T(8,128)} fusion(f32[32,64,16,1,16]{1,4,3,2,0:T(8,128)S(1)} %get-tuple-element.22, f32[32,64,16,1,16]{1,4,3,2,0:T(8,128)S(1)} %get-tuple-element.21, f32[32,64]{1,0:T(8,128)S(1)} %copy-done.6), kind=kLoop, calls=%fused_computation.12 | loop fusion | flops 2097152 | bytes 8396800 | tf_op jit(solution)/shard_map/mul | solution.py:165
  389.5 21.3 %multiply_add_fusion = f32[32,256,512]{2,1,0:T(8,128)} fusion(f32[32,256,512]{2,1,0:T(8,128)} %copy-done.4, f32[32,64,256]{2,1,0:T(8,128)} %all-gather.5.cloned.1.call-done, f32[512,64,1]{0,1,2:T(8,128)S(1)} %reshape.294, f32[32]{0:T(128)S(1)} %copy-done.7), kind=kOutput, calls=%fused_computation.9 | convolution fusion | flops 3229614080 | bytes 35782784 | tf_op jit(solution)/shard_map/ckh,wk->chw/dot_general | solution.py:144
  (82 shorter events, 14.6 us)
Async XLA Ops:
  7.2 21.7 %copy-start = (s32[64,2]{0,1:T(2,128)S(1)}, s32[64,2]{0,1:T(2,128)}, u32[]{:S(2)}) copy-start(s32[64,2]{0,1:T(2,128)} %param.12) | copy-start | bytes 1540
  7.2 33.9 %reduce-scatter.6.cloned.1.call-start = ((), (), s32[]{:S(2)}) async-start(), calls=%async_computation.5 | async-start | bytes 3145728 | tf_op jit(solution)/shard_map/reduce_scatter | solution.py:130
  7.8 21.3 %copy-start.8 = (s32[64]{0:T(128)S(1)}, s32[64]{0:T(128)}, u32[]{:S(2)}) copy-start(s32[64]{0:T(128)} %param.13) | copy-start | bytes 772
  28.5 42.1 %reduce-scatter.8.cloned.1.call-start = ((), (), s32[]{:S(2)}) async-start(), calls=%async_computation.6 | async-start | bytes 327680 | tf_op jit(solution)/shard_map/reduce_scatter | solution.py:132
  29.2 0.6 copy-start.5
  49.2 72.4 %reduce-scatter.10.cloned.1.call-start = ((), (), s32[]{:S(2)}) async-start(), calls=%async_computation.7 | async-start | bytes 1572864 | tf_op jit(solution)/shard_map/reduce_scatter | solution.py:155
  72.1 17.0 %copy-start.3 = (f32[32,64,16,16]{1,3,2,0:T(8,128)S(1)}, f32[32,64,16,16]{1,3,2,0:T(8,128)}, u32[]{:S(2)}) copy-start(f32[32,64,16,16]{1,3,2,0:T(8,128)} %get-tuple-element.11) | copy-start | bytes 6291460
  72.1 23.1 %copy-start.2 = (f32[32,64,16,16]{1,3,2,0:T(8,128)S(1)}, f32[32,64,16,16]{1,3,2,0:T(8,128)}, u32[]{:S(2)}) copy-start(f32[32,64,16,16]{1,3,2,0:T(8,128)} %get-tuple-element.12) | copy-start | bytes 6291460
  102.8 78.0 %all-gather.3.cloned.1.call-start = ((), (), s32[]{:S(2)}) async-start(), calls=%async_computation.8 | async-start | bytes 3145728 | tf_op jit(solution)/shard_map/all_gather | solution.py:143
  122.7 58.1 %copy-start.7 = (f32[32]{0:T(128)S(1)}, f32[32]{0:T(128)}, u32[]{:S(2)}) copy-start(f32[32]{0:T(128)} %param.10) | copy-start | bytes 388
  122.7 58.1 %copy-start.9 = (f32[32]{0:T(128)S(1)}, f32[32]{0:T(128)}, u32[]{:S(2)}) copy-start(f32[32]{0:T(128)} %param.11) | copy-start | bytes 388
  169.7 82.2 %reduce-scatter.12.cloned.1.call-start = ((), (), s32[]{:S(2)}) async-start(), calls=%async_computation.9 | async-start | bytes 3145728 | tf_op jit(solution)/shard_map/reduce_scatter | solution.py:130
  216.9 6.2 %copy-start.4 = (f32[32,256,512]{2,1,0:T(8,128)}, f32[32,256,512]{2,1,0:T(8,128)S(1)}, u32[]{:S(2)}) copy-start(f32[32,256,512]{2,1,0:T(8,128)S(1)} %get-tuple-element.9) | copy-start | bytes 50331652
  240.9 40.6 %reduce-scatter.14.cloned.1.call-start = ((), (), s32[]{:S(2)}) async-start(), calls=%async_computation.10 | async-start | bytes 327680 | tf_op jit(solution)/shard_map/reduce_scatter | solution.py:132
  260.0 129.5 %all-gather.5.cloned.1.call-start = ((), (), s32[]{:S(2)}) async-start(), calls=%async_computation.11 | async-start | bytes 3145728 | tf_op jit(solution)/shard_map/all_gather | solution.py:143
  339.1 28.6 %copy-start.10 = (f32[32]{0:T(128)S(1)}, f32[32]{0:T(128)}, u32[]{:S(2)}) copy-start(f32[32]{0:T(128)} %get-tuple-element.5) | copy-start | bytes 388
  364.7 20.2 %copy-start.6 = (f32[32,64]{1,0:T(8,128)S(1)}, f32[32,64]{1,0:T(8,128)}, u32[]{:S(2)}) copy-start(f32[32,64]{1,0:T(8,128)} %copy-done.5) | copy-start | bytes 24580
  389.5 21.3 %copy-start.1 = (s32[64,2]{0,1:T(2,128)S(1)}, s32[64,2]{0,1:T(2,128)}, u32[]{:S(2)}) copy-start(s32[64,2]{0,1:T(2,128)} %param.12) | copy-start | bytes 1540
Sparse Core Ops, SparseCore 0:
  28.6 12.3 reduce-scatter.5
  49.3 21.2 reduce-scatter.7
  103.0 18.5 reduce-scatter.9
  169.8 11.0 all-gather.2
  241.0 10.7 reduce-scatter.11
  260.1 21.2 reduce-scatter.13
  367.4 10.3 all-gather.4
where the time goes:
time: 424 us; the launch traced here: 418 us
  matrix products  188 us (44%)
  blocking collectives  84.8 us (20%)
  waiting for transfers between devices  78.2 us (18%)
  local copies, waits for them, and re-layouts  32.6 us (8%)
  other arithmetic  19.1 us (5%)
  between operations  15.1 us (4%)
    all_gather x2, blocking collectives, synthesis(): whole_modes = lax.all_gather(modes_in, 'slab', axis=3, tiled=True)  58.4 us
    dot_general x2, matrix products, synthesis(): return jnp.einsum('ckh,wk->chw', gathered, column_tab, precision=precise)  57.4 us
    dot_general x2, matrix products, spectrum(): jnp.einsum('chw,wk->ckh', values, column_tab, precision=precise)  38.5 us
    reduce_scatter x2, waiting for transfers between devices, spectrum(): lax.psum_scatter(row_forward(paired, row_cos, row_sin), 'slab', scatter_d...  34.8 us
    reduce_scatter x1, waiting for transfers between devices, local(): lax.psum_scatter(contract(spectra, masked_weight), 'chan', scatter_dimens...  18.5 us
    psum x1, blocking collectives, local(): lax.psum((jnp.sum(grad_sum * source_field, axis=(1, 2)), jnp.sum(grad_sum...  14.5 us
    reduce_scatter x2, waiting for transfers between devices, spectrum(): lax.psum_scatter(partial_cols, 'mode', scatter_dimension=1, tiled=True)  13.6 us
    all_gather x1, blocking collectives, local(): all_grads = lax.all_gather(grad_modes, 'chan', axis=0, tiled=True)  11.9 us
  transfers between devices with their start and end apart: 7, of which 6 were waited for; matrix products, arithmetic and copies ran while one was open for 6% of the time, Pallas kernels for 0%

commit v1 on v0

v1 whole, which is shorter than its diff:
```python
import functools
import math

import jax
import jax.numpy as jnp
from jax import lax
from jax.experimental import pallas as pl
from jax.experimental.pallas import tpu as pltpu
from jax.sharding import PartitionSpec as P

LANES = 128
BIG = 60 * 1024 * 1024


def split_table(table):
    high = lax.reduce_precision(table, 8, 7)
    return high.astype(jnp.bfloat16), (table - high).astype(jnp.bfloat16)


def split_block(values):
    high = values.astype(jnp.bfloat16)
    return high, (values - high.astype(jnp.float32)).astype(jnp.bfloat16)


def dot_pair(left, right):
    left_high, left_low = left
    right_high, right_low = right
    mul = functools.partial(jnp.dot, preferred_element_type=jnp.float32)
    return mul(left_high, right_high) + mul(left_low, right_high) + mul(left_high, right_low)


def tables(extent, waves, first_cell, cell_count):
    cell_index = first_cell + jnp.arange(cell_count, dtype=jnp.int32)
    products = (cell_index[:, None] * waves[None, :] % extent).astype(jnp.float32)
    angles = products * (2.0 * math.pi / extent)
    return jnp.cos(angles), jnp.sin(angles)


def store_spectrum(values, col_pair, row_pair, out_ref):
    block, rows, cols = values.shape
    lines = dot_pair(split_block(values.reshape(block * rows, cols)), col_pair)
    kx = row_pair[0].shape[0] // 2
    half = lines.shape[1] // 2
    for c in range(block):
        mixed = dot_pair(row_pair, split_block(lines[c * rows : (c + 1) * rows]))
        sines = mixed[kx:]
        out_ref[c] = mixed[:kx] + jnp.concatenate([sines[:, half:], -sines[:, :half]], axis=1)


def synth(modes, row_pair, col_pair):
    half = modes.shape[1] // 2
    turned = jnp.concatenate([-modes[:, half:], modes[:, :half]], axis=1)
    stacked = jnp.concatenate([modes, turned], axis=0)
    lines = dot_pair(row_pair, split_block(stacked))
    return dot_pair(split_block(lines), col_pair)


def spectrum_kernel(x_ref, ch_ref, cl_ref, rh_ref, rl_ref, out_ref):
    store_spectrum(x_ref[...], (ch_ref[...], cl_ref[...]), (rh_ref[...], rl_ref[...]), out_ref)


def middle_kernel(
    x_ref, cot_ref, modes_ref, gain_ref, bias_ref, ch_ref, cl_ref, rh_ref, rl_ref,
    cth_ref, ctl_ref, ih_ref, il_ref, out_ref, grad_ref, spec_ref, sums_ref,
):
    block = x_ref.shape[0]
    row_back = (ih_ref[...], il_ref[...])
    col_back = (cth_ref[...], ctl_ref[...])
    scale = math.sqrt(2.0 / math.pi)
    for c in range(block):
        source = x_ref[c]
        gain = gain_ref[c]
        v = synth(modes_ref[c], row_back, col_back) + gain[:, :1] * source + bias_ref[c][:, :1]
        square = v * v
        t = jnp.tanh(scale * v * (1.0 + 0.044715 * square))
        half_up = 0.5 * (1.0 + t)
        out_ref[c] = v * half_up
        slope = half_up + 0.5 * v * (1.0 - t * t) * (scale * (1.0 + 3.0 * 0.044715 * square))
        grad = cot_ref[c] * slope
        grad_ref[c] = grad
        gate = jnp.sum(jnp.sum(grad * source, axis=0, keepdims=True), axis=1, keepdims=True)
        bias = jnp.sum(jnp.sum(grad, axis=0, keepdims=True), axis=1, keepdims=True)
        lane = lax.broadcasted_iota(jnp.int32, (1, LANES), 1)
        sums_ref[c] = jnp.where(lane == 0, gate, bias)
    store_spectrum(
        grad_ref[...], (ch_ref[...], cl_ref[...]), (rh_ref[...], rl_ref[...]), spec_ref
    )


def last_kernel(grad_ref, modes_ref, gain_ref, cth_ref, ctl_ref, ih_ref, il_ref, out_ref):
    for c in range(grad_ref.shape[0]):
        branch = synth(modes_ref[c], (ih_ref[...], il_ref[...]), (cth_ref[...], ctl_ref[...]))
        out_ref[c] = branch + gain_ref[c][:, :1] * grad_ref[c]


def contract_kernel(w_ref, spec_ref, limit_ref, out_ref):
    block, freqs, _, kx, outs = w_ref.shape
    first = lax.axis_index("chan") * (block * pl.num_programs(0)) + pl.program_id(0) * block

    @pl.when(pl.program_id(0) == 0)
    def _():
        out_ref[...] = jnp.zeros_like(out_ref)

    limit = limit_ref[...]
    for y in range(freqs):
        real = out_ref[y, 0]
        imag = out_ref[y, 1]
        for i in range(block):
            keep = first + i < limit
            spec = spec_ref[i]
            s_real = jnp.where(keep, spec[:, y : y + 1], 0.0)
            s_imag = jnp.where(keep, spec[:, freqs + y : freqs + y + 1], 0.0)
            w_real = w_ref[i, y, 0]
            w_imag = w_ref[i, y, 1]
            real = real + (s_real * w_real - s_imag * w_imag)
            imag = imag + (s_real * w_imag + s_imag * w_real)
        out_ref[y, 0] = real
        out_ref[y, 1] = imag


def back_kernel(w_ref, spec_ref, grads_ref, limit_ref, wgrad_ref, out_ref):
    block, freqs, _, kx, outs = w_ref.shape
    first = lax.axis_index("chan") * (block * pl.num_programs(0)) + pl.program_id(0) * block
    limit = limit_ref[...]
    lane = lax.broadcasted_iota(jnp.int32, (kx, 2 * freqs), 1)

    def one(i, carry):
        keep = first + i < limit
        spec = spec_ref[i]
        back = jnp.zeros((kx, 2 * freqs), jnp.float32)
        for y in range(freqs):
            g_real = jnp.where(keep, grads_ref[y, 0], 0.0)
            g_imag = jnp.where(keep, grads_ref[y, 1], 0.0)
            s_real = spec[:, y : y + 1]
            s_imag = spec[:, freqs + y : freqs + y + 1]
            wgrad_ref[i, y, 0] = s_real * g_real + s_imag * g_imag
            wgrad_ref[i, y, 1] = s_real * g_imag - s_imag * g_real
            w_real = w_ref[i, y, 0]
            w_imag = w_ref[i, y, 1]
            b_real = jnp.sum(g_real * w_real + g_imag * w_imag, axis=1, keepdims=True)
            b_imag = jnp.sum(g_imag * w_real - g_real * w_imag, axis=1, keepdims=True)
            back = jnp.where(lane == y, b_real, back)
            back = jnp.where(lane == freqs + y, b_imag, back)
        out_ref[i] = back
        return carry

    lax.fori_loop(0, block, one, 0)


def exchange_kernel(axes, sizes, gather, x_ref, out_ref, send_sem, recv_sem, own_sem):
    total = math.prod(sizes)
    me = lax.axis_index(axes[0])
    for axis, size in zip(axes[1:], sizes[1:]):
        me = me * size + lax.axis_index(axis)

    def place(index):
        coords = {}
        for axis, size in reversed(list(zip(axes, sizes))):
            coords[axis] = lax.rem(index, size)
            index = lax.div(index, size)
        return coords

    barrier = pltpu.get_barrier_semaphore()
    for step in range(1, total):
        pl.semaphore_signal(
            barrier, inc=1, device_id=place(lax.rem(me + step, total)),
            device_id_type=pl.DeviceIdType.MESH,
        )
    pl.semaphore_wait(barrier, total - 1)
    copies = []
    for step in range(1, total):
        peer = lax.rem(me + step, total)
        copy = pltpu.make_async_remote_copy(
            src_ref=x_ref if gather else x_ref.at[peer],
            dst_ref=out_ref.at[me],
            send_sem=send_sem.at[step],
            recv_sem=recv_sem.at[step],
            device_id=place(peer),
            device_id_type=pl.DeviceIdType.MESH,
        )
        copy.start()
        copies.append(copy)
    own = pltpu.make_async_copy(x_ref if gather else x_ref.at[me], out_ref.at[me], own_sem)
    own.start()
    own.wait()
    for copy in copies:
        copy.wait()


def exchange(values, axes, gather, ident):
    sizes = tuple(lax.axis_size(axis) for axis in axes)
    total = math.prod(sizes)
    piece = values.shape if gather else values.shape[1:]
    flat = values.reshape((-1, LANES) if gather else (total, -1, LANES))
    out = pl.pallas_call(
        functools.partial(exchange_kernel, axes, sizes, gather),
        out_shape=jax.ShapeDtypeStruct((total,) + flat.shape[-2:], jnp.float32),
        in_specs=[pl.BlockSpec(memory_space=pltpu.VMEM)],
        out_specs=pl.BlockSpec(memory_space=pltpu.VMEM),
        scratch_shapes=[
            pltpu.SemaphoreType.DMA((total,)),
            pltpu.SemaphoreType.DMA((total,)),
            pltpu.SemaphoreType.DMA,
        ],
        compiler_params=pltpu.CompilerParams(collective_id=ident, has_side_effects=True),
        name="exchange" + str(ident),
    )(flat)
    return out.reshape((total,) + piece)


def mode_weights(limit_rows, col_freq, row_freq, kx_count, cells_total):
    keep_cols = col_freq[None, :] < limit_rows[:, 0:1]
    keep_rows = (row_freq[None, :] < limit_rows[:, 1:2]) | (
        (kx_count - row_freq)[None, :] < limit_rows[:, 1:2]
    )
    scales = jnp.where(col_freq == 0, 1.0, 2.0).astype(jnp.float32) / cells_total
    joined = keep_rows[:, :, None] & keep_cols[:, None, :]
    return (joined.astype(jnp.float32) * scales[None, None, :])[:, :, None, :]


def local(
    source_field, cotangent, spectral_weight, skip_gain, channel_bias, mode_limit, width_limit
):
    channels, row_count, col_count = source_field.shape
    slabs = lax.axis_size("slab")
    modes = lax.axis_size("mode")
    chans = lax.axis_size("chan")
    slab_index = lax.axis_index("slab")
    mode_index = lax.axis_index("mode")
    chan_index = lax.axis_index("chan")
    outs = spectral_weight.shape[1]
    freqs = spectral_weight.shape[2]
    kx = spectral_weight.shape[4]
    all_freqs = freqs * modes
    all_kx = kx * slabs
    all_rows = row_count * slabs
    all_cols = col_count * modes

    col_waves = jnp.arange(all_freqs, dtype=jnp.int32)
    row_waves = jnp.arange(all_kx, dtype=jnp.int32)
    row_waves = row_waves + jnp.where(2 * row_waves >= all_kx, all_rows - all_kx, 0)
    col_cos, col_sin = tables(all_cols, col_waves, mode_index * col_count, col_count)
    row_cos, row_sin = tables(all_rows, row_waves, slab_index * row_count, row_count)
    col_tab = jnp.concatenate([col_cos, -col_sin], axis=1)
    row_tab = jnp.concatenate([row_cos, row_sin], axis=1)
    col_pair = split_table(col_tab)
    col_back = tuple(part.T for part in col_pair)
    row_back = split_table(row_tab)
    row_pair = tuple(part.T for part in row_back)

    block = 2
    cells = pl.BlockSpec((block, row_count, col_count), lambda c: (c, 0, 0))
    freq_cells = pl.BlockSpec((block, all_kx, 2 * all_freqs), lambda c: (c, 0, 0))
    per_channel = pl.BlockSpec((block, 1, LANES), lambda c: (c, 0, 0))
    field = jax.ShapeDtypeStruct(source_field.shape, jnp.float32)
    freq_field = jax.ShapeDtypeStruct((channels, all_kx, 2 * all_freqs), jnp.float32)
    params = pltpu.CompilerParams(
        dimension_semantics=("arbitrary",), vmem_limit_bytes=BIG
    )

    def whole(array):
        return pl.BlockSpec(array.shape, lambda c: (0,) * array.ndim)

    grid = (channels // block,)
    wide = lambda values: jnp.broadcast_to(values[:, None, None], (channels, 1, LANES))
    gain = wide(skip_gain)
    forward = col_pair + row_pair
    back = col_back + row_back

    def spread(partial, ident):
        cut = partial.reshape(channels, slabs, kx, 2, modes, freqs).transpose(1, 4, 0, 2, 3, 5)
        cut = cut.reshape(slabs * modes, channels, kx, 2 * freqs)
        return jnp.sum(exchange(cut, ("slab", "mode"), False, ident), axis=0)

    def joined(parts):
        parts = parts.reshape(slabs, modes, channels, kx, 2, freqs)
        return parts.transpose(2, 0, 3, 4, 1, 5).reshape(channels, all_kx, 2 * all_freqs)

    spectra = spread(
        pl.pallas_call(
            spectrum_kernel,
            grid=grid,
            in_specs=[cells] + [whole(t) for t in forward],
            out_specs=freq_cells,
            out_shape=freq_field,
            compiler_params=params,
            name="spectrum",
        )(source_field, *forward),
        0,
    )

    weight = spectral_weight.transpose(0, 2, 3, 4, 1)
    limit = width_limit.reshape(1, outs)
    in_block = 4
    w_spec = pl.BlockSpec((in_block, freqs, 2, kx, outs), lambda i: (i, 0, 0, 0, 0))
    s_spec = pl.BlockSpec((in_block, kx, 2 * freqs), lambda i: (i, 0, 0))
    mode_spec = pl.BlockSpec((freqs, 2, kx, outs), lambda i: (0, 0, 0, 0))
    limit_spec = pl.BlockSpec((1, outs), lambda i: (0, 0))
    partial_modes = pl.pallas_call(
        contract_kernel,
        grid=(channels // in_block,),
        in_specs=[w_spec, s_spec, limit_spec],
        out_specs=mode_spec,
        out_shape=jax.ShapeDtypeStruct((freqs, 2, kx, outs), jnp.float32),
        compiler_params=params,
        name="contract",
    )(weight, spectra, limit)
    halves = partial_modes.transpose(3, 2, 1, 0).reshape(chans, channels, kx, 2 * freqs)
    summed_modes = jnp.sum(exchange(halves, ("chan",), False, 1), axis=0)

    col_freq = mode_index * freqs + jnp.arange(freqs, dtype=jnp.int32)
    row_freq = slab_index * kx + jnp.arange(kx, dtype=jnp.int32)
    limit_rows = lax.dynamic_slice_in_dim(mode_limit, chan_index * channels, channels, 0)
    weights = mode_weights(limit_rows, col_freq, row_freq, all_kx, all_rows * all_cols)
    weights = jnp.broadcast_to(weights, (channels, kx, 2, freqs)).reshape(
        channels, kx, 2 * freqs
    )
    out_modes = joined(exchange(summed_modes * weights, ("slab", "mode"), True, 2))

    output, grad_sum, grad_partial, sums = pl.pallas_call(
        middle_kernel,
        grid=grid,
        in_specs=[cells, cells, freq_cells, per_channel, per_channel]
        + [whole(t) for t in forward + back],
        out_specs=[cells, cells, freq_cells, per_channel],
        out_shape=[
            field,
            field,
            freq_field,
            jax.ShapeDtypeStruct((channels, 1, LANES), jnp.float32),
        ],
        compiler_params=params,
        name="middle",
    )(source_field, cotangent, out_modes, gain, wide(channel_bias), *forward, *back)

    grad_modes = spread(grad_partial, 3) * weights
    all_grads = exchange(grad_modes, ("chan",), True, 4)
    all_grads = all_grads.reshape(outs, kx, 2, freqs).transpose(3, 2, 1, 0)
    weight_grad, back_modes = pl.pallas_call(
        back_kernel,
        grid=(channels // in_block,),
        in_specs=[w_spec, s_spec, mode_spec, limit_spec],
        out_specs=[w_spec, s_spec],
        out_shape=[
            jax.ShapeDtypeStruct(weight.shape, jnp.float32),
            jax.ShapeDtypeStruct(spectra.shape, jnp.float32),
        ],
        compiler_params=params,
        name="back",
    )(weight, spectra, all_grads, limit)
    spectral_grad = weight_grad.transpose(0, 4, 1, 2, 3)

    sent = back_modes.size // LANES
    row_sums = sums[:, 0, :2].T.reshape(-1)
    extra = -(-row_sums.size // (8 * LANES)) * 8
    row_sums = jnp.pad(row_sums, (0, extra * LANES - row_sums.size)).reshape(extra, LANES)
    packed = jnp.concatenate([back_modes.reshape(sent, LANES), row_sums], axis=0)
    parts = exchange(packed, ("slab", "mode"), True, 5)
    field_modes = joined(parts[:, :sent])
    totals = jnp.sum(parts[:, sent:], axis=0).reshape(-1)
    gate_grad = totals[:channels]
    bias_grad = totals[channels : 2 * channels]
    field_grad = pl.pallas_call(
        last_kernel,
        grid=grid,
        in_specs=[cells, freq_cells, per_channel] + [whole(t) for t in back],
        out_specs=cells,
        out_shape=field,
        compiler_params=params,
        name="last",
    )(grad_sum, field_modes, gain, *back)
    return (output, field_grad, spectral_grad, gate_grad, bias_grad)


def solution(mesh):
    in_specs = (
        P(("member", "chan"), "slab", "mode"),
        P(("member", "chan"), "slab", "mode"),
        P(("member", "chan"), None, "mode", None, "slab"),
        P(("member", "chan")),
        P(("member", "chan")),
        P("member", None),
        P("member"),
    )
    out_specs = (
        P(("member", "chan"), "slab", "mode"),
        P(("member", "chan"), "slab", "mode"),
        P(("member", "chan"), None, "mode", None, "slab"),
        P(("member", "chan")),
        P(("member", "chan")),
    )
    return jax.shard_map(local, mesh=mesh, in_specs=in_specs, out_specs=out_specs, check_vma=False)
```

time: 424 us -> 287 us (0.68)
  Pallas kernels: 0 us -> 198 us
  matrix products: 188 us -> 0 us
  blocking collectives: 84.8 us -> 0 us
  waiting for transfers between devices: 78.2 us -> 0 us
  local copies, waits for them, and re-layouts: 32.6 us -> 77.1 us
  between operations: 15.1 us -> 0.91 us
  other arithmetic: 19.1 us -> 7 us
    pallas_call x0 -> x11, Pallas kernels: none -> 198 us  [the longest x6 77.7 us: exchange(): pl.pallas_call(functools.partial(exchange_kernel, axes, sizes, gather), o...]
    dot_general x28 -> x0, matrix products: 188 us -> none  [the longest x2 57.4 us: synthesis(): return jnp.einsum('ckh,wk->chw', gathered, column_tab, precision=precise)]
    all_gather x3 -> x0, blocking collectives: 70.3 us -> none  [the longest x2 58.4 us: synthesis(): whole_modes = lax.all_gather(modes_in, 'slab', axis=3, tiled=True)]
    reduce_scatter x5 -> x0, waiting for transfers between devices: 66.9 us -> none  [the longest x2 34.8 us: spectrum(): lax.psum_scatter(row_forward(paired, row_cos, row_sin), 'slab', scatter_d...]
    transpose x0 -> x7, local copies, waits for them, and re-layouts: none -> 25.2 us  [the longest x2 10.9 us: joined(): parts.transpose(2, 0, 3, 4, 1, 5).reshape(channels, all_kx, 2 * all_freqs)]
    another operation x4 -> x6, local copies, waits for them, and re-layouts: 3.07 us -> 27.7 us  [the longest x3 16.6 us: exchange(): flat = values.reshape((-1, LANES) if gather else (total, -1, LANES))]
    psum x1 -> x0, blocking collectives: 14.5 us -> none  [local(): lax.psum((jnp.sum(grad_sum * source_field, axis=(1, 2)), jnp.sum(grad_sum...]
    mul x5 -> x3, other arithmetic: 14.4 us -> 1.41 us  [the longest x1 0.64 us: local(): summed_modes * weights]
  transfers between devices with their start and end apart: 7 -> 0, of which waited for: 6 -> 0; matrix products, arithmetic and copies ran while one was open for 6% -> 0% of each run, Pallas kernels for 0% -> 0%
where the time goes in v1:
time: 287 us; the launch traced here: 283 us
  Pallas kernels  198 us (69%)
  local copies, waits for them, and re-layouts  77.1 us (27%)
  other arithmetic  7 us (2%)
    pallas_call x6, Pallas kernels, exchange(): pl.pallas_call(functools.partial(exchange_kernel, axes, sizes, gather), o...  77.7 us
    pallas_call x1, Pallas kernels, local(): pl.pallas_call(middle_kernel, grid=grid, in_specs=[cells, cells, freq_cel...  45.7 us
    pallas_call x1, Pallas kernels, local(): pl.pallas_call(back_kernel, grid=(channels // in_block,), in_specs=[w_spe...  23.5 us
    pallas_call x1, Pallas kernels, local(): pl.pallas_call(last_kernel, grid=grid, in_specs=[cells, freq_cells, per_c...  22.6 us
    pallas_call x1, Pallas kernels, local(): pl.pallas_call(spectrum_kernel, grid=grid, in_specs=[cells] + [whole(t) f...  20.1 us
    another operation x3, local copies, waits for them, and re-layouts, exchange(): flat = values.reshape((-1, LANES) if gather else (total, -1, LANES))  16.6 us
    transpose x2, local copies, waits for them, and re-layouts, joined(): parts.transpose(2, 0, 3, 4, 1, 5).reshape(channels, all_kx, 2 * all_freqs)  10.9 us
    transpose x2, local copies, waits for them, and re-layouts, spread(): partial.reshape(channels, slabs, kx, 2, modes, freqs)  10.8 us

profile of v1, /device:TPU:0, one launch (start us, length us, event | category | flops | bytes accessed | tf_op | source)
XLA Modules:
  0.0 283.0 jit_solution(7245887412592074954)
XLA Ops:
  0.7 0.7 copy-done
  1.5 1.4 broadcast_in_dim.27.gain_ref
  2.9 1.3 broadcast_in_dim.28.bias_ref
  4.6 0.7 copy.27.cl_ref
  5.3 0.8 copy.26.ch_ref
  6.2 0.6 fusion.9
  6.9 0.7 copy.28.rh_ref
  7.7 0.7 copy.29.rl_ref
  8.7 0.7 reshape.184
  9.3 20.1 %spectrum.1 = f32[32,64,64]{2,1,0:T(8,128)} custom-call(f32[32,256,512]{2,1,0:T(8,128)} %x_ref.3, bf16[512,64]{1,0:T(8,128)(2,1)} %copy.26.ch_ref, bf16[512,64]{1,0:T(8,128)(2,1)} %copy.27.cl_ref, bf16[128,256]{1,0:T(8,128)(2,1)} %copy.28.rh_ref, bf16[128,256]{1,0:T(8,128)(2,1)} %copy.29.rl_ref), custom_call_target="tpu_custom_call" | custom-call | tf_op jit(solution)/shard_map/spectrum/pallas_call | solution.py:280
  29.5 1.9 copy.30
  31.4 5.4 %copy.31 = f32[4,2,32,16,2,16]{5,4,3,2,1,0:T(2,128)} copy(f32[4,2,32,16,2,16]{2,5,1,4,3,0:T(8,128)S(1)} %bitcast.34) | data formatting | bytes 1048576 | tf_op jit(solution)/shard_map/transpose | solution.py:271
  36.8 7.3 %reshape_reshape.15.x_ref = f32[8,128,128]{2,1,0:T(8,128)} reshape(f32[4,2,32,16,2,16]{5,4,3,2,1,0:T(2,128)} %copy.31) | data formatting | bytes 1048576 | tf_op jit(solution)/shard_map/reshape;reshape | solution.py:194
  44.1 16.0 %exchange0.1 = f32[8,128,128]{2,1,0:T(8,128)} custom-call(f32[8,128,128]{2,1,0:T(8,128)} %reshape_reshape.15.x_ref), custom_call_target="tpu_custom_call" | custom-call | tf_op jit(solution)/shard_map/exchange0/pallas_call | solution.py:195
  60.1 1.1 reduce_sum.38
  61.2 0.8 reduce_sum.39.spec_ref
  62.0 8.3 %contract.1 = f32[16,2,16,64]{3,2,1,0:T(8,128)} custom-call(f32[32,16,2,16,64]{4,3,2,1,0:T(8,128)} %bitcast.30, f32[32,16,32]{2,1,0:T(8,128)} %reduce_sum.39.spec_ref, s32[1,64]{1,0:T(1,128)} %bitcast.48), custom_call_target="tpu_custom_call" | custom-call | tf_op jit(solution)/shard_map/contract/pallas_call | solution.py:299
  70.3 2.0 copy.32
  72.4 2.0 reshape_reshape.16.x_ref
  74.3 6.4 %exchange1.1 = f32[2,128,128]{2,1,0:T(8,128)} custom-call(f32[2,128,128]{2,1,0:T(8,128)} %reshape_reshape.16.x_ref), custom_call_target="tpu_custom_call" | custom-call | tf_op jit(solution)/shard_map/exchange1/pallas_call | solution.py:195
  80.7 0.9 reduce_sum.40
  81.6 0.6 mul.98.x_ref
  82.3 15.9 %exchange2.1 = f32[8,128,128]{2,1,0:T(8,128)} custom-call(f32[128,128]{1,0:T(8,128)} %mul.98.x_ref), custom_call_target="tpu_custom_call" | custom-call | tf_op jit(solution)/shard_map/exchange2/pallas_call | solution.py:195
  98.2 7.7 %reshape_reshape.17 = f32[4,2,32,16,2,16]{5,4,3,2,1,0:T(2,128)} reshape(f32[8,128,128]{2,1,0:T(8,128)} %exchange2.1) | data formatting | bytes 1048576 | tf_op jit(solution)/shard_map/reshape;reshape | solution.py:276
  105.9 5.5 %copy.33 = f32[32,4,16,2,2,16]{0,5,4,3,2,1:T(8,128)S(1)} copy(f32[32,4,16,2,2,16]{5,3,2,0,4,1:T(2,128)} %bitcast.32) | data formatting | bytes 1048576 | tf_op jit(solution)/shard_map/transpose | solution.py:277
  111.4 1.7 copy.34.modes_ref
  113.1 45.7 %middle.1 = (f32[32,256,512]{2,1,0:T(8,128)}, f32[32,256,512]{2,1,0:T(8,128)}, f32[32,64,64]{2,1,0:T(8,128)}, f32[32,1,128]{2,1,0:T(1,128)}) custom-call(f32[32,256,512]{2,1,0:T(8,128)} %x_ref.3, f32[32,256,512]{2,1,0:T(8,128)} %cot_ref.1, f32[32,64,64]{2,1,0:T(8,128)} %copy.34.modes_ref, f32[32,1,128]{2,1,0:T(1,128)} %broadcast_in_dim.27.gain_ref, ...), custom_call_target="tpu_custom_call" | custom-call | tf_op jit(solution)/shard_map/middle/pallas_call | solution.py:320
  158.9 0.8 copy.42
  159.7 1.9 copy.39
  161.6 5.4 %copy.40 = f32[4,2,32,16,2,16]{5,4,3,2,1,0:T(2,128)} copy(f32[4,2,32,16,2,16]{2,5,1,4,3,0:T(8,128)S(1)} %bitcast.36) | data formatting | bytes 1048576 | tf_op jit(solution)/shard_map/transpose | solution.py:271
  167.0 7.3 %reshape_reshape.18.x_ref = f32[8,128,128]{2,1,0:T(8,128)} reshape(f32[4,2,32,16,2,16]{5,4,3,2,1,0:T(2,128)} %copy.40) | data formatting | bytes 1048576 | tf_op jit(solution)/shard_map/reshape;reshape | solution.py:194
  174.3 16.5 %exchange3.1 = f32[8,128,128]{2,1,0:T(8,128)} custom-call(f32[8,128,128]{2,1,0:T(8,128)} %reshape_reshape.18.x_ref), custom_call_target="tpu_custom_call" | custom-call | tf_op jit(solution)/shard_map/exchange3/pallas_call | solution.py:195
  190.9 1.1 reduce_sum.41
  191.9 0.6 mul.99.x_ref
  192.6 6.4 %exchange4.1 = f32[2,128,128]{2,1,0:T(8,128)} custom-call(f32[128,128]{1,0:T(8,128)} %mul.99.x_ref), custom_call_target="tpu_custom_call" | custom-call | tf_op jit(solution)/shard_map/exchange4/pallas_call | solution.py:195
  199.0 2.2 reshape_reshape.19
  201.2 1.2 copy.41
  202.4 23.5 %back.1 = (f32[32,16,2,16,64]{4,3,2,1,0:T(8,128)}, f32[32,16,32]{2,1,0:T(8,128)}) custom-call(f32[32,16,2,16,64]{4,3,2,1,0:T(8,128)} %bitcast.31, f32[32,16,32]{2,1,0:T(8,128)} %reduce_sum.39.spec_ref, f32[16,2,16,64]{3,2,1,0:T(8,128)} %bitcast.44, s32[1,64]{1,0:T(1,128)} %bitcast.49), custom_call_target="tpu_custom_call" | custom-call | tf_op jit(solution)/shard_map/back/pallas_call | solution.py:339
  225.9 1.1 reshape.187
  227.0 0.6 pad_maximum_fusion.2.x_ref
  227.6 16.5 %exchange5.1 = f32[8,136,128]{2,1,0:T(8,128)} custom-call(f32[136,128]{1,0:T(8,128)} %pad_maximum_fusion.2.x_ref), custom_call_target="tpu_custom_call" | custom-call | tf_op jit(solution)/shard_map/exchange5/pallas_call | solution.py:195
  244.1 0.8 slice_reduce_fusion
  244.9 1.1 slice.28
  245.9 0.6 fusion.15
  246.5 6.7 %reshape.190 = f32[4,2,32,16,2,16]{5,4,3,2,1,0:T(2,128)} reshape(f32[8,128,128]{2,1,0:T(8,128)S(1)} %slice.28) | data formatting | bytes 1048576 | tf_op jit(solution)/shard_map/reshape | solution.py:276
  253.2 5.5 %copy.43 = f32[32,4,16,2,2,16]{0,5,4,3,2,1:T(8,128)S(1)} copy(f32[32,4,16,2,2,16]{5,3,2,0,4,1:T(2,128)} %bitcast.33) | data formatting | bytes 1048576 | tf_op jit(solution)/shard_map/transpose | solution.py:277
  258.7 1.7 copy.44.modes_ref
  260.4 22.6 %last.1 = f32[32,256,512]{2,1,0:T(8,128)} custom-call(f32[32,256,512]{2,1,0:T(8,128)} %get-tuple-element.12.grad_ref, f32[32,64,64]{2,1,0:T(8,128)} %copy.44.modes_ref, f32[32,1,128]{2,1,0:T(1,128)} %broadcast_in_dim.27.gain_ref, bf16[64,512]{1,0:T(8,128)(2,1)} %bitcast.41, bf16[64,512]{1,0:T(8,128)(2,1)} %bitcast.39, bf16[256,128]{1,0:T(8,128)(2,1)} %copy-done.5, ...), custom_call_target="tpu_custom_call" | custom-call | tf_op jit(solution)/shard_map/last/pallas_call | solution.py:363
  (28 shorter events, 1.1 us)
Async XLA Ops:
  0.6 0.7 copy-start
  4.6 24.9 %copy-start.2 = (bf16[512,64]{0,1:T(8,128)(2,1)}, bf16[512,64]{0,1:T(8,128)(2,1)S(1)}, u32[]{:S(2)}) copy-start(bf16[512,64]{0,1:T(8,128)(2,1)S(1)} %get-tuple-element.19) | copy-start | bytes 196612
  4.6 24.9 %copy-start.3 = (bf16[512,64]{0,1:T(8,128)(2,1)}, bf16[512,64]{0,1:T(8,128)(2,1)S(1)}, u32[]{:S(2)}) copy-start(bf16[512,64]{0,1:T(8,128)(2,1)S(1)} %get-tuple-element.20) | copy-start | bytes 196612
  6.9 22.6 %copy-start.4 = (bf16[256,128]{1,0:T(8,128)(2,1)}, bf16[256,128]{1,0:T(8,128)(2,1)S(1)}, u32[]{:S(2)}) copy-start(bf16[256,128]{1,0:T(8,128)(2,1)S(1)} %get-tuple-element.17.il_ref) | copy-start | bytes 196612
  6.9 22.6 %copy-start.5 = (bf16[256,128]{1,0:T(8,128)(2,1)}, bf16[256,128]{1,0:T(8,128)(2,1)S(1)}, u32[]{:S(2)}) copy-start(bf16[256,128]{1,0:T(8,128)(2,1)S(1)} %get-tuple-element.18.ih_ref) | copy-start | bytes 196612
  260.4 22.6 %copy-start.1 = (s32[64,2]{0,1:T(2,128)S(1)}, s32[64,2]{0,1:T(2,128)}, u32[]{:S(2)}) copy-start(s32[64,2]{0,1:T(2,128)} %param.12) | copy-start | bytes 1540

commit v2 on v1

--- a/solution.py
+++ b/solution.py
@@ -39,18 +39,43 @@
 def store_spectrum(values, col_pair, row_pair, out_ref):
     block, rows, cols = values.shape
     lines = dot_pair(split_block(values.reshape(block * rows, cols)), col_pair)
-    kx = row_pair[0].shape[0] // 2
-    half = lines.shape[1] // 2
+    all_kx = row_pair[0].shape[0] // 2
+    kx, lanes = out_ref.shape[2:]
+    span = lanes // block
+    mode_count = lines.shape[1] // span
+    slabs = out_ref.shape[0] // mode_count
+    done = []
     for c in range(block):
         mixed = dot_pair(row_pair, split_block(lines[c * rows : (c + 1) * rows]))
-        sines = mixed[kx:]
-        out_ref[c] = mixed[:kx] + jnp.concatenate([sines[:, half:], -sines[:, :half]], axis=1)
-
-
-def synth(modes, row_pair, col_pair):
-    half = modes.shape[1] // 2
-    turned = jnp.concatenate([-modes[:, half:], modes[:, :half]], axis=1)
-    stacked = jnp.concatenate([modes, turned], axis=0)
+        done.append(mixed[:all_kx] - turn(mixed[all_kx:], span))
+    for m in range(mode_count):
+        packed = jnp.concatenate([one[:, m * span : (m + 1) * span] for one in done], axis=1)
+        for s in range(slabs):
+            out_ref[m * slabs + s, 0] = packed[s * kx : (s + 1) * kx]
+
+
+def turn(values, span):
+    half = span // 2
+    pieces = []
+    for first in range(0, values.shape[1], span):
+        pieces.append(-values[:, first + half : first + span])
+        pieces.append(values[:, first : first + half])
+    return jnp.concatenate(pieces, axis=1)
+
+
+def all_modes(modes_ref, mode_count, c, block):
+    span = modes_ref.shape[3] // block
+    slabs = modes_ref.shape[0] // mode_count
+    columns = []
+    for m in range(mode_count):
+        stack = [modes_ref[m * slabs + s, 0] for s in range(slabs)]
+        columns.append(jnp.concatenate(stack, axis=0)[:, c * span : (c + 1) * span])
+    return jnp.concatenate(columns, axis=1), span
+
+
+def synth(modes_and_span, row_pair, col_pair):
+    modes, span = modes_and_span
+    stacked = jnp.concatenate([modes, turn(modes, span)], axis=0)
     lines = dot_pair(row_pair, split_block(stacked))
     return dot_pair(split_block(lines), col_pair)
 
@@ -60,7 +85,7 @@
 
 
 def middle_kernel(
-    x_ref, cot_ref, modes_ref, gain_ref, bias_ref, ch_ref, cl_ref, rh_ref, rl_ref,
+    mode_count, x_ref, cot_ref, modes_ref, gain_ref, bias_ref, ch_ref, cl_ref, rh_ref, rl_ref,
     cth_ref, ctl_ref, ih_ref, il_ref, out_ref, grad_ref, spec_ref, sums_ref,
 ):
     block = x_ref.shape[0]
@@ -70,7 +95,7 @@
     for c in range(block):
         source = x_ref[c]
         gain = gain_ref[c]
-        v = synth(modes_ref[c], row_back, col_back) + gain[:, :1] * source + bias_ref[c][:, :1]
+        v = synth(all_modes(modes_ref, mode_count, c, block), row_back, col_back) + gain[:, :1] * source + bias_ref[c][:, :1]
         square = v * v
         t = jnp.tanh(scale * v * (1.0 + 0.044715 * square))
         half_up = 0.5 * (1.0 + t)
@@ -87,9 +112,11 @@
     )
 
 
-def last_kernel(grad_ref, modes_ref, gain_ref, cth_ref, ctl_ref, ih_ref, il_ref, out_ref):
-    for c in range(grad_ref.shape[0]):
-        branch = synth(modes_ref[c], (ih_ref[...], il_ref[...]), (cth_ref[...], ctl_ref[...]))
+def last_kernel(mode_count, grad_ref, modes_ref, gain_ref, cth_ref, ctl_ref, ih_ref, il_ref, out_ref):
+    block = grad_ref.shape[0]
+    for c in range(block):
+        modes = all_modes(modes_ref, mode_count, c, block)
+        branch = synth(modes, (ih_ref[...], il_ref[...]), (cth_ref[...], ctl_ref[...]))
         out_ref[c] = branch + gain_ref[c][:, :1] * grad_ref[c]
 
 
@@ -107,9 +134,10 @@
         imag = out_ref[y, 1]
         for i in range(block):
             keep = first + i < limit
-            spec = spec_ref[i]
-            s_real = jnp.where(keep, spec[:, y : y + 1], 0.0)
-            s_imag = jnp.where(keep, spec[:, freqs + y : freqs + y + 1], 0.0)
+            spec = spec_ref[0]
+            at = 2 * freqs * i + y
+            s_real = jnp.where(keep, spec[:, at : at + 1], 0.0)
+            s_imag = jnp.where(keep, spec[:, freqs + at : freqs + at + 1], 0.0)
             w_real = w_ref[i, y, 0]
             w_imag = w_ref[i, y, 1]
             real = real + (s_real * w_real - s_imag * w_imag)
@@ -122,29 +150,26 @@
     block, freqs, _, kx, outs = w_ref.shape
     first = lax.axis_index("chan") * (block * pl.num_programs(0)) + pl.program_id(0) * block
     limit = limit_ref[...]
-    lane = lax.broadcasted_iota(jnp.int32, (kx, 2 * freqs), 1)
-
-    def one(i, carry):
+    lane = lax.broadcasted_iota(jnp.int32, out_ref.shape[1:], 1)
+    spec = spec_ref[0]
+    back = jnp.zeros(out_ref.shape[1:], jnp.float32)
+    for i in range(block):
         keep = first + i < limit
-        spec = spec_ref[i]
-        back = jnp.zeros((kx, 2 * freqs), jnp.float32)
         for y in range(freqs):
+            at = 2 * freqs * i + y
             g_real = jnp.where(keep, grads_ref[y, 0], 0.0)
             g_imag = jnp.where(keep, grads_ref[y, 1], 0.0)
-            s_real = spec[:, y : y + 1]
-            s_imag = spec[:, freqs + y : freqs + y + 1]
+            s_real = spec[:, at : at + 1]
+            s_imag = spec[:, freqs + at : freqs + at + 1]
             wgrad_ref[i, y, 0] = s_real * g_real + s_imag * g_imag
             wgrad_ref[i, y, 1] = s_real * g_imag - s_imag * g_real
             w_real = w_ref[i, y, 0]
             w_imag = w_ref[i, y, 1]
             b_real = jnp.sum(g_real * w_real + g_imag * w_imag, axis=1, keepdims=True)
             b_imag = jnp.sum(g_imag * w_real - g_real * w_imag, axis=1, keepdims=True)
-            back = jnp.where(lane == y, b_real, back)
-            back = jnp.where(lane == freqs + y, b_imag, back)
-        out_ref[i] = back
-        return carry
-
-    lax.fori_loop(0, block, one, 0)
+            back = jnp.where(lane == at, b_real, back)
+            back = jnp.where(lane == freqs + at, b_imag, back)
+    out_ref[0] = back
 
 
 def exchange_kernel(axes, sizes, gather, x_ref, out_ref, send_sem, recv_sem, own_sem):
@@ -241,19 +266,23 @@
     row_waves = row_waves + jnp.where(2 * row_waves >= all_kx, all_rows - all_kx, 0)
     col_cos, col_sin = tables(all_cols, col_waves, mode_index * col_count, col_count)
     row_cos, row_sin = tables(all_rows, row_waves, slab_index * row_count, row_count)
-    col_tab = jnp.concatenate([col_cos, -col_sin], axis=1)
+    col_tab = jnp.stack(
+        [col_cos.reshape(-1, modes, freqs), -col_sin.reshape(-1, modes, freqs)], axis=2
+    ).reshape(col_count, 2 * all_freqs)
     row_tab = jnp.concatenate([row_cos, row_sin], axis=1)
     col_pair = split_table(col_tab)
     col_back = tuple(part.T for part in col_pair)
     row_back = split_table(row_tab)
     row_pair = tuple(part.T for part in row_back)
 
-    block = 2
+    block = LANES // (2 * freqs)
+    groups = channels // block
+    owners = slabs * modes
     cells = pl.BlockSpec((block, row_count, col_count), lambda c: (c, 0, 0))
-    freq_cells = pl.BlockSpec((block, all_kx, 2 * all_freqs), lambda c: (c, 0, 0))
+    freq_cells = pl.BlockSpec((owners, 1, kx, LANES), lambda c: (0, c, 0, 0))
     per_channel = pl.BlockSpec((block, 1, LANES), lambda c: (c, 0, 0))
     field = jax.ShapeDtypeStruct(source_field.shape, jnp.float32)
-    freq_field = jax.ShapeDtypeStruct((channels, all_kx, 2 * all_freqs), jnp.float32)
+    freq_field = jax.ShapeDtypeStruct((owners, groups, kx, LANES), jnp.float32)
     params = pltpu.CompilerParams(
         dimension_semantics=("arbitrary",), vmem_limit_bytes=BIG
     )
@@ -268,13 +297,15 @@
     back = col_back + row_back
 
     def spread(partial, ident):
-        cut = partial.reshape(channels, slabs, kx, 2, modes, freqs).transpose(1, 4, 0, 2, 3, 5)
-        cut = cut.reshape(slabs * modes, channels, kx, 2 * freqs)
-        return jnp.sum(exchange(cut, ("slab", "mode"), False, ident), axis=0)
-
-    def joined(parts):
-        parts = parts.reshape(slabs, modes, channels, kx, 2, freqs)
-        return parts.transpose(2, 0, 3, 4, 1, 5).reshape(channels, all_kx, 2 * all_freqs)
+        half = exchange(partial.reshape(modes, -1, LANES), ("mode",), False, ident)
+        half = jnp.sum(half, axis=0).reshape(slabs, -1, LANES)
+        return jnp.sum(exchange(half, ("slab",), False, ident + 1), axis=0).reshape(
+            groups, kx, LANES
+        )
+
+    def joined(piece, ident):
+        half = exchange(piece, ("slab",), True, ident)
+        return exchange(half, ("mode",), True, ident + 1).reshape((owners,) + piece.shape)
 
     spectra = spread(
         pl.pallas_call(
@@ -291,9 +322,9 @@
 
     weight = spectral_weight.transpose(0, 2, 3, 4, 1)
     limit = width_limit.reshape(1, outs)
-    in_block = 4
+    in_block = block
     w_spec = pl.BlockSpec((in_block, freqs, 2, kx, outs), lambda i: (i, 0, 0, 0, 0))
-    s_spec = pl.BlockSpec((in_block, kx, 2 * freqs), lambda i: (i, 0, 0))
+    s_spec = pl.BlockSpec((1, kx, LANES), lambda i: (i, 0, 0))
     mode_spec = pl.BlockSpec((freqs, 2, kx, outs), lambda i: (0, 0, 0, 0))
     limit_spec = pl.BlockSpec((1, outs), lambda i: (0, 0))
     partial_modes = pl.pallas_call(
@@ -305,20 +336,21 @@
         compiler_params=params,
         name="contract",
     )(weight, spectra, limit)
-    halves = partial_modes.transpose(3, 2, 1, 0).reshape(chans, channels, kx, 2 * freqs)
-    summed_modes = jnp.sum(exchange(halves, ("chan",), False, 1), axis=0)
+    halves = partial_modes.reshape(freqs, 2, kx, chans, groups, block)
+    halves = halves.transpose(3, 4, 2, 5, 1, 0).reshape(chans, groups, kx, LANES)
+    summed_modes = jnp.sum(exchange(halves, ("chan",), False, 2), axis=0)
 
     col_freq = mode_index * freqs + jnp.arange(freqs, dtype=jnp.int32)
     row_freq = slab_index * kx + jnp.arange(kx, dtype=jnp.int32)
     limit_rows = lax.dynamic_slice_in_dim(mode_limit, chan_index * channels, channels, 0)
     weights = mode_weights(limit_rows, col_freq, row_freq, all_kx, all_rows * all_cols)
-    weights = jnp.broadcast_to(weights, (channels, kx, 2, freqs)).reshape(
-        channels, kx, 2 * freqs
-    )
-    out_modes = joined(exchange(summed_modes * weights, ("slab", "mode"), True, 2))
+    weights = jnp.broadcast_to(weights, (channels, kx, 2, freqs))
+    weights = weights.reshape(groups, block, kx, 2 * freqs).transpose(0, 2, 1, 3)
+    weights = weights.reshape(groups, kx, LANES)
+    out_modes = joined(summed_modes * weights, 3)
 
     output, grad_sum, grad_partial, sums = pl.pallas_call(
-        middle_kernel,
+        functools.partial(middle_kernel, modes),
         grid=grid,
         in_specs=[cells, cells, freq_cells, per_channel, per_channel]
         + [whole(t) for t in forward + back],
@@ -333,9 +365,10 @@
         name="middle",
     )(source_field, cotangent, out_modes, gain, wide(channel_bias), *forward, *back)
 
-    grad_modes = spread(grad_partial, 3) * weights
-    all_grads = exchange(grad_modes, ("chan",), True, 4)
-    all_grads = all_grads.reshape(outs, kx, 2, freqs).transpose(3, 2, 1, 0)
+    grad_modes = spread(grad_partial, 5) * weights
+    all_grads = exchange(grad_modes, ("chan",), True, 7)
+    all_grads = all_grads.reshape(chans, groups, kx, block, 2, freqs)
+    all_grads = all_grads.transpose(5, 4, 2, 0, 1, 3).reshape(freqs, 2, kx, outs)
     weight_grad, back_modes = pl.pallas_call(
         back_kernel,
         grid=(channels // in_block,),
@@ -355,13 +388,13 @@
     extra = -(-row_sums.size // (8 * LANES)) * 8
     row_sums = jnp.pad(row_sums, (0, extra * LANES - row_sums.size)).reshape(extra, LANES)
     packed = jnp.concatenate([back_modes.reshape(sent, LANES), row_sums], axis=0)
-    parts = exchange(packed, ("slab", "mode"), True, 5)
-    field_modes = joined(parts[:, :sent])
+    parts = joined(packed, 8)
+    field_modes = parts[:, :sent].reshape(owners, groups, kx, LANES)
     totals = jnp.sum(parts[:, sent:], axis=0).reshape(-1)
     gate_grad = totals[:channels]
     bias_grad = totals[channels : 2 * channels]
     field_grad = pl.pallas_call(
-        last_kernel,
+        functools.partial(last_kernel, modes),
         grid=grid,
         in_specs=[cells, freq_cells, per_channel] + [whole(t) for t in back],
         out_specs=cells,

time: 287 us -> 208 us (0.72); the launches traced: 283 us -> 207 us
  local copies, waits for them, and re-layouts: 77.1 us -> 18.8 us
  Pallas kernels: 198 us -> 175 us
  other arithmetic: 7 us -> 11.9 us
    transpose x5 -> x2, local copies, waits for them, and re-layouts: 23.8 us -> 0.91 us  [the longest x1 0.8 us: local(): halves.transpose(3, 4, 2, 5, 1, 0).reshape(chans, groups, kx, LANES)]
    another operation x3 -> x1, local copies, waits for them, and re-layouts: 16.6 us -> 1.95 us  [exchange(): flat = values.reshape((-1, LANES) if gather else (total, -1, LANES))]
    pallas_call x6 -> x10, Pallas kernels: 77.7 us -> 67.3 us  [exchange(): pl.pallas_call(functools.partial(exchange_kernel, axes, sizes, gather), o...]
    reshape x5 -> x3, local copies, waits for them, and re-layouts: 11.9 us -> 1.66 us  [the longest x1 1.2 us: local(): all_grads.transpose(5, 4, 2, 0, 1, 3).reshape(freqs, 2, kx, outs)]
    pallas_call x2, Pallas kernels: 68.3 us -> 59.9 us  [the longest x1 41.4 us: local(): pl.pallas_call(functools.partial(middle_kernel, modes), grid=grid, in_spe...]
    another operation x3 -> x2, local copies, waits for them, and re-layouts: 11.1 us -> 2.75 us  [local(): all_grads = all_grads.reshape(chans, groups, kx, block, 2, freqs)]
    pallas_call x1, Pallas kernels: 20.1 us -> 15.8 us  [local(): pl.pallas_call(spectrum_kernel, grid=grid, in_specs=[cells] + [whole(t) f...]
    reduce_sum x3 -> x5, other arithmetic: 3.08 us -> 7.09 us  [the longest x2 3.6 us: spread(): half = jnp.sum(half, axis=0).reshape(slabs, -1, LANES)]
where the time goes in v2:
time: 208 us; the launch traced here: 207 us
  Pallas kernels  175 us (84%)
  local copies, waits for them, and re-layouts  18.8 us (9%)
  other arithmetic  11.9 us (6%)
    pallas_call x10, Pallas kernels, exchange(): pl.pallas_call(functools.partial(exchange_kernel, axes, sizes, gather), o...  67.3 us
    pallas_call x1, Pallas kernels, local(): pl.pallas_call(functools.partial(middle_kernel, modes), grid=grid, in_spe...  41.4 us
    pallas_call x1, Pallas kernels, local(): pl.pallas_call(back_kernel, grid=(channels // in_block,), in_specs=[w_spe...  24 us
    pallas_call x1, Pallas kernels, local(): pl.pallas_call(functools.partial(last_kernel, modes), grid=grid, in_specs...  18.4 us
    pallas_call x1, Pallas kernels, local(): pl.pallas_call(spectrum_kernel, grid=grid, in_specs=[cells] + [whole(t) f...  15.8 us
    pallas_call x1, Pallas kernels, local(): pl.pallas_call(contract_kernel, grid=(channels // in_block,), in_specs=[w...  8.39 us

profile of v2, /device:TPU:0, one launch (start us, length us, event | category | flops | bytes accessed | tf_op | source)
XLA Modules:
  0.0 207.0 jit_solution(7463916735803346383)
XLA Ops:
  0.7 0.7 copy-done
  1.6 1.4 broadcast_in_dim.27.gain_ref
  2.9 1.3 broadcast_in_dim.28.bias_ref
  4.3 0.3 fusion.10
  4.7 0.8 copy.24.cl_ref
  5.4 0.8 copy.23.ch_ref
  6.2 0.1 and_select_fusion
  6.3 0.6 fusion.9
  6.9 0.1 fusion.1
  7.1 0.7 copy.25.rh_ref
  7.8 0.7 copy.26.rl_ref
  8.5 0.3 broadcast_in_dim.26
  8.8 0.3 reshape.298
  9.1 0.1 copy.29
  9.2 0.2 reshape.299
  9.4 15.8 %spectrum.1 = f32[8,8,16,128]{3,2,1,0:T(8,128)} custom-call(f32[32,256,512]{2,1,0:T(8,128)} %x_ref.3, bf16[512,64]{1,0:T(8,128)(2,1)} %copy.23.ch_ref, bf16[512,64]{1,0:T(8,128)(2,1)} %copy.24.cl_ref, bf16[128,256]{1,0:T(8,128)(2,1)} %copy.25.rh_ref, bf16[128,256]{1,0:T(8,128)(2,1)} %copy.26.rl_ref), custom_call_target="tpu_custom_call" | custom-call | tf_op jit(solution)/shard_map/spectrum/pallas_call | solution.py:311
  25.1 3.6 %exchange0.1 = f32[2,512,128]{2,1,0:T(8,128)} custom-call(f32[2,512,128]{2,1,0:T(8,128)} %bitcast.47), custom_call_target="tpu_custom_call" | custom-call | tf_op jit(solution)/shard_map/exchange0/pallas_call | solution.py:220
  28.7 1.8 reduce_sum.54
  30.5 12.1 %exchange1.1 = f32[4,128,128]{2,1,0:T(8,128)} custom-call(f32[4,128,128]{2,1,0:T(8,128)} %bitcast.57), custom_call_target="tpu_custom_call" | custom-call | tf_op jit(solution)/shard_map/exchange1/pallas_call | solution.py:220
  42.6 1.6 reduce_sum.55
  44.2 8.4 %contract.1 = f32[16,2,16,64]{3,2,1,0:T(8,128)} custom-call(f32[32,16,2,16,64]{4,3,2,1,0:T(8,128)} %bitcast.39, f32[8,16,128]{2,1,0:T(8,128)} %bitcast.59, s32[1,64]{1,0:T(1,128)} %bitcast.65), custom_call_target="tpu_custom_call" | custom-call | tf_op jit(solution)/shard_map/contract/pallas_call | solution.py:330
  52.6 1.4 copy.27
  54.1 0.8 copy.28
  54.9 2.0 reshape_reshape.15.x_ref
  56.8 5.8 %exchange2.1 = f32[2,128,128]{2,1,0:T(8,128)} custom-call(f32[2,128,128]{2,1,0:T(8,128)} %reshape_reshape.15.x_ref), custom_call_target="tpu_custom_call" | custom-call | tf_op jit(solution)/shard_map/exchange2/pallas_call | solution.py:220
  62.7 0.9 reduce_sum.56
  63.6 0.6 mul.133.x_ref
  64.3 9.6 %exchange3.1 = f32[4,128,128]{2,1,0:T(8,128)} custom-call(f32[128,128]{1,0:T(8,128)} %mul.133.x_ref), custom_call_target="tpu_custom_call" | custom-call | tf_op jit(solution)/shard_map/exchange3/pallas_call | solution.py:220
  73.8 3.3 %exchange4.1 = f32[2,512,128]{2,1,0:T(8,128)} custom-call(f32[512,128]{1,0:T(8,128)} %bitcast.55), custom_call_target="tpu_custom_call" | custom-call | tf_op jit(solution)/shard_map/exchange4/pallas_call | solution.py:220
  77.2 41.4 %middle.1 = (f32[32,256,512]{2,1,0:T(8,128)}, f32[32,256,512]{2,1,0:T(8,128)}, f32[8,8,16,128]{3,2,1,0:T(8,128)}, f32[32,1,128]{2,1,0:T(1,128)}) custom-call(f32[32,256,512]{2,1,0:T(8,128)} %x_ref.3, f32[32,256,512]{2,1,0:T(8,128)} %cot_ref.1, f32[8,8,16,128]{3,2,1,0:T(8,128)} %bitcast.45, f32[32,1,128]{2,1,0:T(1,128)} %broadcast_in_dim.27.gain_ref, ...), custom_call_target="tpu_custom_call" | custom-call | tf_op jit(solution)/shard_map/middle/pallas_call | solution.py:352
  118.6 0.8 copy.36
  119.5 3.4 %exchange5.1 = f32[2,512,128]{2,1,0:T(8,128)} custom-call(f32[2,512,128]{2,1,0:T(8,128)} %bitcast.61), custom_call_target="tpu_custom_call" | custom-call | tf_op jit(solution)/shard_map/exchange5/pallas_call | solution.py:220
  122.9 1.8 reduce_sum.57
  124.7 10.5 %exchange6.1 = f32[4,128,128]{2,1,0:T(8,128)} custom-call(f32[4,128,128]{2,1,0:T(8,128)} %bitcast.58), custom_call_target="tpu_custom_call" | custom-call | tf_op jit(solution)/shard_map/exchange6/pallas_call | solution.py:220
  135.3 1.0 reduce_sum.58
  136.3 0.6 mul.134.x_ref
  136.9 5.8 %exchange7.1 = f32[2,128,128]{2,1,0:T(8,128)} custom-call(f32[128,128]{1,0:T(8,128)} %mul.134.x_ref), custom_call_target="tpu_custom_call" | custom-call | tf_op jit(solution)/shard_map/exchange7/pallas_call | solution.py:220
  142.7 2.2 %reshape_reshape.18 = f32[2,8,16,4,2,16]{5,4,3,2,1,0:T(2,128)S(1)} reshape(f32[2,128,128]{2,1,0:T(8,128)} %exchange7.1) | data formatting | bytes 262144 | tf_op jit(solution)/shard_map/reshape;reshape | solution.py:370
  144.9 0.5 copy.34
  145.5 1.2 copy.35.grads_ref
  146.7 24.0 %back.1 = (f32[32,16,2,16,64]{4,3,2,1,0:T(8,128)}, f32[8,16,128]{2,1,0:T(8,128)}) custom-call(f32[32,16,2,16,64]{4,3,2,1,0:T(8,128)} %bitcast.40, f32[8,16,128]{2,1,0:T(8,128)} %bitcast.60, f32[16,2,16,64]{3,2,1,0:T(8,128)} %copy.35.grads_ref, s32[1,64]{1,0:T(1,128)} %bitcast.66), custom_call_target="tpu_custom_call" | custom-call | tf_op jit(solution)/shard_map/back/pallas_call | solution.py:372
  170.7 1.5 pad_maximum_fusion.2.x_ref
  172.2 9.8 %exchange8.1 = f32[4,136,128]{2,1,0:T(8,128)} custom-call(f32[136,128]{1,0:T(8,128)} %pad_maximum_fusion.2.x_ref), custom_call_target="tpu_custom_call" | custom-call | tf_op jit(solution)/shard_map/exchange8/pallas_call | solution.py:220
  181.9 3.4 %exchange9.1 = f32[2,544,128]{2,1,0:T(8,128)} custom-call(f32[544,128]{1,0:T(8,128)} %bitcast.48), custom_call_target="tpu_custom_call" | custom-call | tf_op jit(solution)/shard_map/exchange9/pallas_call | solution.py:220
  185.3 0.8 slice_reduce_fusion
  186.1 1.9 slice.32
  187.9 18.4 %last.1 = f32[32,256,512]{2,1,0:T(8,128)} custom-call(f32[32,256,512]{2,1,0:T(8,128)} %get-tuple-element.12.grad_ref, f32[8,8,16,128]{3,2,1,0:T(8,128)} %bitcast.46, f32[32,1,128]{2,1,0:T(1,128)} %broadcast_in_dim.27.gain_ref, bf16[64,512]{1,0:T(8,128)(2,1)} %bitcast.52, bf16[64,512]{1,0:T(8,128)(2,1)} %bitcast.50, bf16[256,128]{1,0:T(8,128)(2,1)} %copy-done.5, ...), custom_call_target="tpu_custom_call" | custom-call | tf_op jit(solution)/shard_map/last/pallas_call | solution.py:396
  206.4 0.6 fusion.12
  (26 shorter events, 0.3 us)
Async XLA Ops:
  0.6 0.7 copy-start
  4.6 49.4 %copy-start.2 = (bf16[512,64]{0,1:T(8,128)(2,1)}, bf16[512,64]{0,1:T(8,128)(2,1)S(1)}, u32[]{:S(2)}) copy-start(bf16[512,64]{0,1:T(8,128)(2,1)S(1)} %get-tuple-element.19) | copy-start | bytes 196612
  4.7 49.4 %copy-start.3 = (bf16[512,64]{0,1:T(8,128)(2,1)}, bf16[512,64]{0,1:T(8,128)(2,1)S(1)}, u32[]{:S(2)}) copy-start(bf16[512,64]{0,1:T(8,128)(2,1)S(1)} %get-tuple-element.20) | copy-start | bytes 196612
  7.0 47.8 %copy-start.4 = (bf16[256,128]{1,0:T(8,128)(2,1)}, bf16[256,128]{1,0:T(8,128)(2,1)S(1)}, u32[]{:S(2)}) copy-start(bf16[256,128]{1,0:T(8,128)(2,1)S(1)} %get-tuple-element.17.il_ref) | copy-start | bytes 196612
  7.0 47.8 %copy-start.5 = (bf16[256,128]{1,0:T(8,128)(2,1)}, bf16[256,128]{1,0:T(8,128)(2,1)S(1)}, u32[]{:S(2)}) copy-start(bf16[256,128]{1,0:T(8,128)(2,1)S(1)} %get-tuple-element.18.ih_ref) | copy-start | bytes 196612
  187.9 19.0 %copy-start.1 = (s32[64,2]{0,1:T(2,128)S(1)}, s32[64,2]{0,1:T(2,128)}, u32[]{:S(2)}) copy-start(s32[64,2]{0,1:T(2,128)} %param.12) | copy-start | bytes 1540
